TPU v7x, 32 devices: a whole 2x2x4 slice. The times are simulated.
32 devices in a mesh: dev: 32 (over z, y, x, core).
Axes of the slice: x: 2, y: 2, z: 4, core: 2. Of those that a mesh axis runs over, the one named last changes fastest.
Arguments:
- pixels: bfloat16 [96, 64, 16], P('dev'), may hold values from -6 to 6
- embed_w: bfloat16 [96, 16, 8192], P('dev'), may hold values from -1.5 to 1.5
- var_embed: bfloat16 [96, 8192], P('dev'), may hold values from -3 to 3
- key_w: bfloat16 [8192, 8192], P('dev'), may hold values from -0.0625 to 0.0625
- query: float32 [8192], replicated, may hold values from -500 to 500
- value_t: bfloat16 [8192, 8192], P('dev'), may hold values from -0.0625 to 0.0625
- out_w: bfloat16 [8192, 8192], P('dev'), may hold values from -0.0625 to 0.0625
Outputs:
- mixed: bfloat16 [64, 8192], P('dev')
All inputs are finite; a program needn't handle non-finite values.
Results may differ from a plain program's by a relative error of at most 0.012.
The roundings to bfloat16 on the way count: a program that leaves them out, or rounds other values in their place, can miss the bound.
Values may be sent and summed in bfloat16 or wider, within the bound.
A program may use at most 64 MiB of HBM per device.

v0:
```python
import jax
import jax.numpy as jnp
from jax import lax
from jax.sharding import PartitionSpec as P

D = 8192
HEADS = 64
HD = 128
V = 91


def body(pixels, embed_w, var_embed, key_w, query, value_t, out_w):
    group_size = lax.axis_size("dev")
    own_embed = jnp.einsum("vtp,vpd->vtd", pixels, embed_w, preferred_element_type=jnp.float32)
    own_embed = (own_embed + var_embed.astype(jnp.float32)[:, None, :]).astype(jnp.bfloat16)
    grouped = lax.all_to_all(own_embed, "dev", split_axis=1, concat_axis=0, tiled=True)
    key_rows = key_w.shape[0]
    keyq_part = jnp.einsum(
        "dhj,hj->dh",
        key_w.astype(jnp.float32).reshape(key_rows, HEADS, HD),
        query.reshape(HEADS, HD),
        precision=lax.Precision.HIGHEST,
    )
    keyq = lax.all_gather(keyq_part, "dev", axis=0, tiled=True)
    logits = jnp.einsum(
        "vtd,dh->vth", grouped.astype(jnp.float32), keyq, precision=lax.Precision.HIGHEST
    ) / jnp.sqrt(jnp.float32(HD))
    slot = lax.broadcasted_iota(jnp.int32, logits.shape, 0)
    logits = jnp.where(slot < V, logits, -1e30)
    row_max = jnp.max(logits, axis=0, keepdims=True)
    weights = jnp.exp(logits - row_max)
    attn = (weights / jnp.sum(weights, axis=0, keepdims=True)).astype(jnp.bfloat16)
    pooled = jnp.einsum("vth,vtd->thd", attn, grouped, preferred_element_type=jnp.float32).astype(
        jnp.bfloat16
    )
    own_tokens = pooled.shape[0]
    if group_size >= HEADS:
        spread = jnp.repeat(pooled, group_size // HEADS, axis=1)[:, :, None, :]
    else:
        spread = pooled.reshape(own_tokens, group_size, HEADS // group_size, D)
    received = lax.all_to_all(spread, "dev", split_axis=1, concat_axis=0, tiled=True)
    all_tokens = received.shape[0]
    head_share = received.shape[2]
    received = received.reshape(all_tokens, head_share, D)
    columns = value_t.shape[0]
    value_heads = jnp.einsum(
        "thd,hcd->thc",
        received,
        value_t.reshape(head_share, columns // head_share, D),
        preferred_element_type=jnp.float32,
    )
    value_heads = value_heads.reshape(all_tokens, columns).astype(jnp.bfloat16)
    summed = lax.psum_scatter(
        jnp.dot(value_heads, out_w, preferred_element_type=jnp.float32),
        "dev",
        scatter_dimension=0,
        tiled=True,
    )
    return summed.astype(jnp.bfloat16)


def solution(mesh):
    placed = (
        P("dev", None, None),
        P("dev", None, None),
        P("dev", None),
        P("dev", None),
        P(),
        P("dev", None),
        P("dev", None),
    )
    return jax.shard_map(
        body, mesh=mesh, in_specs=placed, out_specs=P("dev", None), check_vma=False
    )
```

profile of v0, /device:TPU:0, one launch (start us, length us, event | category | flops | bytes accessed | tf_op | source)
XLA Modules:
  0.0 285.6 jit_solution(11926075932730230169)
XLA Ops:
  6.5 0.9 convert_element_type.26
  7.5 0.2 copy-done
  7.7 1.7 fusion.1
  9.4 4.7 %copy.15 = bf16[3,64,8192]{2,0,1:T(4,128)(2,1)} copy(bf16[3,64,8192]{2,1,0:T(8,128)(2,1)S(1)} %fusion.1) | data formatting | bytes 6291456 | tf_op jit(solution)/shard_map/convert_element_type | solution.py:15
  14.1 7.4 %all-to-all-start = ((bf16[3,64,8192]{2,0,1:T(4,128)(2,1)}), bf16[3,64,8192]{2,0,1:T(4,128)(2,1)}, u32[]{:S(2)}, u32[]{:S(2)}) async-start(bf16[3,64,8192]{2,0,1:T(4,128)(2,1)} %copy.15), calls=%async_computation | async-start | bytes 8388608 | tf_op jit(solution)/shard_map/all_to_all | solution.py:16
  21.6 0.0 copy-start.2
  21.6 0.0 all-gather.2.cloned.1.call-start
  21.6 6.4 %copy.25 = bf16[256,8192]{0,1:T(8,128)(2,1)} copy(bf16[256,8192]{1,0:T(8,128)(2,1)} %param.10) | data formatting | bytes 8388608 | tf_op jit(solution)/shard_map/reshape | solution.py:20
  28.0 3.9 %fusion.32 = f32[64,1,256]{2,1,0:T(1,128)S(1)} fusion(f32[64,128,1]{1,2,0:T(1,128)S(1)} %bitcast.48, bf16[256,64,128]{0,2,1:T(8,128)(2,1)} %bitcast.44), kind=kOutput, calls=%fused_computation.26 | convolution fusion | flops 25165824 | bytes 4292608 | tf_op jit(solution)/shard_map/dhj,hj->dh/dot_general | solution.py:18
  31.9 0.6 copy.47
  32.5 0.0 all-gather.2.cloned.1.call-update
  32.6 93.2 %all-to-all-done = bf16[3,64,8192]{2,0,1:T(4,128)(2,1)} async-done(((bf16[3,64,8192]{2,0,1:T(4,128)(2,1)}), bf16[3,64,8192]{2,0,1:T(4,128)(2,1)}, u32[]{:S(2)}, u32[]{:S(2)}) %all-to-all-start) | async-done | bytes 3145760 | tf_op jit(solution)/shard_map/all_to_all | solution.py:16
  125.8 7.9 %copy.16 = bf16[3,32,2,8192]{3,2,0,1:T(2,128)(2,1)} copy(bf16[3,32,2,8192]{3,0,2,1:T(4,128)(2,1)} %bitcast) | data formatting | bytes 6291456 | tf_op jit(solution)/shard_map/all_to_all | solution.py:16
  133.7 9.0 %fusion.15 = f32[96,2,64]{0,2,1:T(8,128)S(1)} fusion(f32[8192,64]{0,1:T(8,128)} %all-gather.2.cloned.1.call-done, bf16[96,2,8192]{2,1,0:T(2,128)(2,1)} %bitcast.42, pred[96]{0:T(512)(128)(4,1)S(1)} %iota_compare_fusion), kind=kOutput, calls=%fused_computation.13 | convolution fusion | flops 1207984128 | bytes 5292128 | tf_op jit(solution)/shard_map/vtd,dh->vth/dot_general | solution.py:25
  142.7 0.2 fusion.31
  142.9 6.0 %convolution_convert_fusion = bf16[2,64,8192]{2,1,0:T(8,128)(2,1)S(1)} fusion(bf16[96,2,8192]{2,1,0:T(2,128)(2,1)} %bitcast.43, f32[2,64]{1,0:T(2,128)S(1)} %fusion.31, f32[96,2,64]{0,2,1:T(8,128)S(1)} %fusion.15), kind=kOutput, calls=%fused_computation.3 | convolution fusion | flops 202412256 | bytes 5292544 | tf_op jit(solution)/shard_map/vth,vtd->thd/dot_general | solution.py:33
  148.9 2.7 reshape.23
  151.6 6.0 %copy.19 = bf16[2,32,2,8192]{3,2,0,1:T(2,128)(2,1)} copy(bf16[2,32,2,8192]{3,2,1,0:T(2,128)(2,1)} %reshape.23) | data formatting | bytes 4194304 | tf_op jit(solution)/shard_map/reshape | solution.py:40
  157.5 4.1 %all-to-all-start.1 = ((bf16[2,32,2,8192]{3,2,0,1:T(2,128)(2,1)}), bf16[2,32,2,8192]{3,2,0,1:T(2,128)(2,1)S(1)}, u32[]{:S(2)}, u32[]{:S(2)}) async-start(bf16[2,32,2,8192]{3,2,0,1:T(2,128)(2,1)} %copy.19), calls=%async_computation.1 | async-start | bytes 4194304 | tf_op jit(solution)/shard_map/all_to_all | solution.py:41
  161.7 48.7 %all-to-all-done.1 = bf16[2,32,2,8192]{3,2,0,1:T(2,128)(2,1)S(1)} async-done(((bf16[2,32,2,8192]{3,2,0,1:T(2,128)(2,1)}), bf16[2,32,2,8192]{3,2,0,1:T(2,128)(2,1)S(1)}, u32[]{:S(2)}, u32[]{:S(2)}) %all-to-all-start.1) | async-done | bytes 2097184 | tf_op jit(solution)/shard_map/all_to_all | solution.py:41
  210.4 4.1 %fusion.23 = bf16[2,8,8,128]{3,2,1,0:T(8,128)(2,1)S(1)} fusion(bf16[2,128,8192]{2,1,0:T(8,128)(2,1)} %bitcast.46, bf16[64,2,8192]{2,1,0:T(2,128)(2,1)S(1)} %bitcast.45), kind=kOutput, calls=%fused_computation.15 | convolution fusion | flops 268451840 | bytes 6324224 | tf_op jit(solution)/shard_map/thd,hcd->thc/dot_general | solution.py:46
  214.5 0.8 fusion.26
  215.4 61.8 %all-reduce.2 = bf16[64,8192]{1,0:T(8,128)(2,1)} all-reduce(f32[64,8192]{1,0:T(8,128)S(1)} %fusion.26), channel_id=2, replica_groups=mesh['dev'=32] {'dev'}, use_global_device_ids=true, to_apply=%region_2.3.clone | all-reduce | flops 524288 | bytes 3145728
  277.2 1.6 dynamic-slice_convert_fusion
  (6 shorter events, 0.0 us)
Async XLA Ops:
  6.5 1.2 copy-start
  14.1 111.7 %all-to-all-start = ((bf16[3,64,8192]{2,0,1:T(4,128)(2,1)}), bf16[3,64,8192]{2,0,1:T(4,128)(2,1)}, u32[]{:S(2)}, u32[]{:S(2)}) async-start(bf16[3,64,8192]{2,0,1:T(4,128)(2,1)} %copy.15), calls=%async_computation | async-start | bytes 8388608 | tf_op jit(solution)/shard_map/all_to_all | solution.py:16
  21.6 6.4 %copy-start.2 = (f32[8192]{0:T(1024)S(1)}, f32[8192]{0:T(1024)}, u32[]{:S(2)}) copy-start(f32[8192]{0:T(1024)} %param.11) | copy-start | bytes 98308
  21.6 112.1 %all-gather.2.cloned.1.call-start = ((), (), s32[]{:S(2)}) async-start(), calls=%async_computation.2 | async-start | bytes 2162688 | tf_op jit(solution)/shard_map/all_gather | solution.py:24
  157.5 52.9 %all-to-all-start.1 = ((bf16[2,32,2,8192]{3,2,0,1:T(2,128)(2,1)}), bf16[2,32,2,8192]{3,2,0,1:T(2,128)(2,1)S(1)}, u32[]{:S(2)}, u32[]{:S(2)}) async-start(bf16[2,32,2,8192]{3,2,0,1:T(2,128)(2,1)} %copy.19), calls=%async_computation.1 | async-start | bytes 4194304 | tf_op jit(solution)/shard_map/all_to_all | solution.py:41
  210.4 4.1 %copy-start.1 = (bf16[256,8192]{1,0:T(8,128)(2,1)S(1)}, bf16[256,8192]{1,0:T(8,128)(2,1)}, u32[]{:S(2)}) copy-start(bf16[256,8192]{1,0:T(8,128)(2,1)} %param.13) | copy-start | bytes 12582916
Sparse Core Ops, SparseCore 0:
  32.7 79.4 all-gather.1
where the time goes:
time: 286 us
  waiting for transfers between devices  142 us (50%)
  blocking collectives  61.8 us (22%)
  local copies, waits for them, and re-layouts  30 us (10%)
  matrix products  25.6 us (9%)
  between operations  13.5 us (5%)
  starting transfers between devices  11.6 us (4%)
    all_to_all x1, waiting for transfers between devices, body(): lax.all_to_all(own_embed, 'dev', split_axis=1, concat_axis=0, tiled=True)  93.2 us
    unnamed x1, blocking collectives  61.8 us
    all_to_all x1, waiting for transfers between devices, body(): lax.all_to_all(spread, 'dev', split_axis=1, concat_axis=0, tiled=True)  48.7 us
    dot_general x1, matrix products, body(): jnp.einsum('vtd,dh->vth', grouped.astype(jnp.float32), keyq, precision=la...  8.99 us
    reshape x2, local copies, waits for them, and re-layouts, body(): spread = pooled.reshape(own_tokens, group_size, HEADS // group_size, D)  8.65 us
    all_to_all x1, local copies, waits for them, and re-layouts, body(): lax.all_to_all(own_embed, 'dev', split_axis=1, concat_axis=0, tiled=True)  7.92 us
    all_to_all x1, starting transfers between devices, body(): lax.all_to_all(own_embed, 'dev', split_axis=1, concat_axis=0, tiled=True)  7.44 us
    reshape x1, local copies, waits for them, and re-layouts, body(): key_w.astype(jnp.float32).reshape(key_rows, HEADS, HD)  6.36 us
  transfers between devices with their start and end apart: 3, of which 2 were waited for; matrix products, arithmetic and copies ran while one was open for 7% of the time, Pallas kernels for 0%

commit v1 on v0

--- a/solution.py
+++ b/solution.py
@@ -13,7 +13,10 @@
     group_size = lax.axis_size("dev")
     own_embed = jnp.einsum("vtp,vpd->vtd", pixels, embed_w, preferred_element_type=jnp.float32)
     own_embed = (own_embed + var_embed.astype(jnp.float32)[:, None, :]).astype(jnp.bfloat16)
-    grouped = lax.all_to_all(own_embed, "dev", split_axis=1, concat_axis=0, tiled=True)
+    grouped = jnp.concatenate(
+        lax.all_to_all(jnp.stack(jnp.split(own_embed, lax.axis_size("dev"), axis=1)), "dev", 0, 0),
+        axis=0,
+    )
     key_rows = key_w.shape[0]
     keyq_part = jnp.einsum(
         "dhj,hj->dh",

time: 286 us -> 275 us (0.962)
  waiting for transfers between devices: 142 us -> 120 us
  local copies, waits for them, and re-layouts: 30 us -> 40.7 us
    all_to_all x1, waiting for transfers between devices: 93.2 us -> 0.01 us  [body(): lax.all_to_all(jnp.stack(jnp.split(own_embed, lax.axis_size('dev'), axis=...]
    all_gather x1, waiting for transfers between devices: 0.01 us -> 71.1 us  [body(): keyq = lax.all_gather(keyq_part, 'dev', axis=0, tiled=True)]
    unnamed x6 -> x37, local copies, waits for them, and re-layouts: 0.24 us -> 22.7 us
    all_to_all x1 -> x0, local copies, waits for them, and re-layouts: 7.92 us -> none  [body(): lax.all_to_all(own_embed, 'dev', split_axis=1, concat_axis=0, tiled=True)]
    convert_element_type x1 -> x0, local copies, waits for them, and re-layouts: 4.67 us -> none  [body(): (own_embed + var_embed.astype(jnp.float32)[:, None, :]).astype(jnp.bfloat16)]
  transfers between devices with their start and end apart: 3 -> 3, of which waited for: 2 -> 2; matrix products, arithmetic and copies ran while one was open for 7% -> 4% of each run, Pallas kernels for 0% -> 0%
where the time goes in v1:
time: 275 us; the launch traced here: 274 us
  waiting for transfers between devices  120 us (44%)
  blocking collectives  61.8 us (22%)
  local copies, waits for them, and re-layouts  40.7 us (15%)
  matrix products  25.4 us (9%)
  between operations  13.5 us (5%)
  starting transfers between devices  12.1 us (4%)
    all_gather x1, waiting for transfers between devices, body(): keyq = lax.all_gather(keyq_part, 'dev', axis=0, tiled=True)  71.1 us
    unnamed x1, blocking collectives  61.8 us
    all_to_all x1, waiting for transfers between devices, body(): lax.all_to_all(spread, 'dev', split_axis=1, concat_axis=0, tiled=True)  48.7 us
    unnamed x37, local copies, waits for them, and re-layouts  22.7 us
    dot_general x1, matrix products, body(): jnp.einsum('vtd,dh->vth', grouped.astype(jnp.float32), keyq, precision=la...  8.99 us
    reshape x2, local copies, waits for them, and re-layouts, body(): spread = pooled.reshape(own_tokens, group_size, HEADS // group_size, D)  8.66 us
    all_to_all x1, starting transfers between devices, body(): lax.all_to_all(jnp.stack(jnp.split(own_embed, lax.axis_size('dev'), axis=...  7.43 us
    reshape x1, local copies, waits for them, and re-layouts, body(): key_w.astype(jnp.float32).reshape(key_rows, HEADS, HD)  6.4 us
  transfers between devices with their start and end apart: 3, of which 2 were waited for; matrix products, arithmetic and copies ran while one was open for 4% of the time, Pallas kernels for 0%

profile of v1, /device:TPU:0, one launch (start us, length us, event | category | flops | bytes accessed | tf_op | source)
XLA Modules:
  0.0 274.3 jit_solution(15570230848148376057)
XLA Ops:
  6.5 0.9 convert_element_type.26
  7.7 1.7 fusion.1
  11.6 0.7 fusion.54
  15.9 0.7 fusion.48
  16.6 0.8 fusion.47
  17.4 0.7 fusion.46
  18.8 0.7 fusion.44
  23.2 0.7 fusion.38
  26.1 0.7 fusion.34
  31.1 0.7 fusion.27
  32.6 7.4 %all-to-all-start = ((bf16[32,3,2,8192]{3,2,1,0:T(2,128)(2,1)}), bf16[32,3,2,8192]{3,2,1,0:T(2,128)(2,1)}, u32[]{:S(2)}, u32[]{:S(2)}) async-start(bf16[32,3,2,8192]{3,2,1,0:T(2,128)(2,1)} %fusion.26), calls=%async_computation | async-start | bytes 6291456 | tf_op jit(solution)/shard_map/all_to_all | solution.py:17
  40.3 6.4 %copy.23 = bf16[256,8192]{0,1:T(8,128)(2,1)} copy(bf16[256,8192]{1,0:T(8,128)(2,1)} %param.10) | data formatting | bytes 8388608 | tf_op jit(solution)/shard_map/reshape | solution.py:23
  46.7 3.9 %fusion.64 = f32[64,1,256]{2,1,0:T(1,128)S(1)} fusion(f32[64,128,1]{1,2,0:T(1,128)S(1)} %bitcast.171, bf16[256,64,128]{0,2,1:T(8,128)(2,1)} %bitcast.167), kind=kOutput, calls=%fused_computation.90 | convolution fusion | flops 25165824 | bytes 4292608 | tf_op jit(solution)/shard_map/dhj,hj->dh/dot_general | solution.py:21
  51.3 71.1 %all-gather.2.cloned.1.call-done = f32[8192,64]{0,1:T(8,128)} async-done(((f32[256,64]{0,1:T(8,128)}), f32[8192,64]{0,1:T(8,128)}) %all-gather.2.cloned.1.call-update) | async-done | bytes 2097168 | tf_op jit(solution)/shard_map/all_gather | solution.py:27
  122.3 9.0 %fusion.15 = f32[96,2,64]{0,2,1:T(8,128)S(1)} fusion(f32[8192,64]{0,1:T(8,128)} %all-gather.2.cloned.1.call-done, bf16[96,2,8192]{2,1,0:T(2,128)(2,1)} %bitcast.32, pred[96]{0:T(512)(128)(4,1)S(1)} %iota_compare_fusion), kind=kOutput, calls=%fused_computation.13 | convolution fusion | flops 1207984128 | bytes 5292128 | tf_op jit(solution)/shard_map/vtd,dh->vth/dot_general | solution.py:28
  131.5 5.8 %convolution_convert_fusion = bf16[2,64,8192]{2,1,0:T(8,128)(2,1)S(1)} fusion(bf16[96,2,8192]{2,1,0:T(2,128)(2,1)} %bitcast.32, f32[2,64]{1,0:T(2,128)S(1)} %fusion.63, f32[96,2,64]{0,2,1:T(8,128)S(1)} %fusion.15), kind=kOutput, calls=%fused_computation.3 | convolution fusion | flops 202412256 | bytes 5292544 | tf_op jit(solution)/shard_map/vth,vtd->thd/dot_general | solution.py:36
  137.3 2.7 reshape.27
  140.0 6.0 %copy.17 = bf16[2,32,2,8192]{3,2,0,1:T(2,128)(2,1)} copy(bf16[2,32,2,8192]{3,2,1,0:T(2,128)(2,1)} %reshape.27) | data formatting | bytes 4194304 | tf_op jit(solution)/shard_map/reshape | solution.py:43
  146.0 4.4 %all-to-all-start.1 = ((bf16[2,32,2,8192]{3,2,0,1:T(2,128)(2,1)}), bf16[2,32,2,8192]{3,2,0,1:T(2,128)(2,1)S(1)}, u32[]{:S(2)}, u32[]{:S(2)}) async-start(bf16[2,32,2,8192]{3,2,0,1:T(2,128)(2,1)} %copy.17), calls=%async_computation.1 | async-start | bytes 4194304 | tf_op jit(solution)/shard_map/all_to_all | solution.py:44
  150.4 48.7 %all-to-all-done.1 = bf16[2,32,2,8192]{3,2,0,1:T(2,128)(2,1)S(1)} async-done(((bf16[2,32,2,8192]{3,2,0,1:T(2,128)(2,1)}), bf16[2,32,2,8192]{3,2,0,1:T(2,128)(2,1)S(1)}, u32[]{:S(2)}, u32[]{:S(2)}) %all-to-all-start.1) | async-done | bytes 2097184 | tf_op jit(solution)/shard_map/all_to_all | solution.py:44
  199.1 4.1 %fusion.23 = bf16[2,8,8,128]{3,2,1,0:T(8,128)(2,1)S(1)} fusion(bf16[2,128,8192]{2,1,0:T(8,128)(2,1)} %bitcast.169, bf16[64,2,8192]{2,1,0:T(2,128)(2,1)S(1)} %bitcast.168), kind=kOutput, calls=%fused_computation.15 | convolution fusion | flops 268451840 | bytes 6324224 | tf_op jit(solution)/shard_map/thd,hcd->thc/dot_general | solution.py:49
  203.2 0.8 fusion.58
  204.1 61.8 %all-reduce.2 = bf16[64,8192]{1,0:T(8,128)(2,1)} all-reduce(f32[64,8192]{1,0:T(8,128)S(1)} %fusion.58), channel_id=2, replica_groups=mesh['dev'=32] {'dev'}, use_global_device_ids=true, to_apply=%region_2.3.clone | all-reduce | flops 524288 | bytes 3145728
  265.9 1.6 dynamic-slice_convert_fusion
  (36 shorter events, 18.6 us)
Async XLA Ops:
  6.5 1.2 copy-start
  32.6 89.7 %all-to-all-start = ((bf16[32,3,2,8192]{3,2,1,0:T(2,128)(2,1)}), bf16[32,3,2,8192]{3,2,1,0:T(2,128)(2,1)}, u32[]{:S(2)}, u32[]{:S(2)}) async-start(bf16[32,3,2,8192]{3,2,1,0:T(2,128)(2,1)} %fusion.26), calls=%async_computation | async-start | bytes 6291456 | tf_op jit(solution)/shard_map/all_to_all | solution.py:17
  40.1 6.6 %copy-start.2 = (f32[8192]{0:T(1024)S(1)}, f32[8192]{0:T(1024)}, u32[]{:S(2)}) copy-start(f32[8192]{0:T(1024)} %param.11) | copy-start | bytes 98308
  40.1 82.3 %all-gather.2.cloned.1.call-start = ((), (), s32[]{:S(2)}) async-start(), calls=%async_computation.2 | async-start | bytes 2162688 | tf_op jit(solution)/shard_map/all_gather | solution.py:27
  146.0 53.1 %all-to-all-start.1 = ((bf16[2,32,2,8192]{3,2,0,1:T(2,128)(2,1)}), bf16[2,32,2,8192]{3,2,0,1:T(2,128)(2,1)S(1)}, u32[]{:S(2)}, u32[]{:S(2)}) async-start(bf16[2,32,2,8192]{3,2,0,1:T(2,128)(2,1)} %copy.17), calls=%async_computation.1 | async-start | bytes 4194304 | tf_op jit(solution)/shard_map/all_to_all | solution.py:44
  199.1 4.1 %copy-start.1 = (bf16[256,8192]{1,0:T(8,128)(2,1)S(1)}, bf16[256,8192]{1,0:T(8,128)(2,1)}, u32[]{:S(2)}) copy-start(bf16[256,8192]{1,0:T(8,128)(2,1)} %param.13) | copy-start | bytes 12582916
Sparse Core Ops, SparseCore 0:
  51.4 70.9 all-gather.1
